TPU v7x, 32 devices: a whole 2x2x4 slice. The times are simulated.
32 devices in a mesh: row: 4 (over x, core), col: 8 (over z, y).
Axes of the slice: x: 2, y: 2, z: 4, core: 2. Of those that a mesh axis runs over, the one named last changes fastest.
Arguments:
- tokens: bfloat16 [16384, 1024], P(('row', 'col')), may hold values from -6 to 6
- expert_ids: int32 [16384, 1], P(('row', 'col')), may hold values from 0 to 31; in each aligned block of 512 rows (0 to 511, 512 to 1023, ...) at most 32 rows name the same one
- gate_prob: float32 [16384], P(('row', 'col')), may hold values from 0.25 to 1
- norm_gain: float32 [1024], replicated, may hold values from 0.1 to 1.9
- weight_in: bfloat16 [32, 1024, 4096], P(('row', 'col')), may hold values from -0.1875 to 0.1875
- weight_out: bfloat16 [32, 4096, 1024], P(('row', 'col')), may hold values from -0.09375 to 0.09375
Outputs:
- mixed: bfloat16 [16384, 1024], P(('row', 'col'))
- routed: int32 [32], P(('row', 'col'))
Inputs may be any that keep to these rules, and one draw needn't show every extreme that they name: `expert_ids`: among the 512 tokens of one device no expert is chosen more than 32 times; some expert is chosen exactly 32 times by some device's tokens.
All inputs are finite; a program needn't handle non-finite values.
Results may differ from a plain program's by a relative error of at most 0.001.
The roundings to bfloat16 on the way count: a program that leaves them out, or rounds other values in their place, can miss the bound.
Values may be sent and summed in bfloat16 or wider, within the bound.
A program may use at most 64 MiB of HBM per device.

v0:
```python
import functools

import jax
import jax.numpy as jnp
from jax import lax
from jax.experimental import pallas as pl
from jax.experimental.pallas import tpu as pltpu
from jax.sharding import PartitionSpec as P

MESH = pl.DeviceIdType.MESH


def bit_xor(a, b, size):
    out, unit = 0, 1
    while unit < size:
        out = out + lax.rem(lax.div(a, unit) + lax.div(b, unit), 2) * unit
        unit *= 2
    return out


def kernel(
    rows, cols, cap, groups, ff_tile, out_tile,
    tokens_ref, ids_row_ref, gain_ref, first_hbm, second_hbm,
    back_ref, routed_ref,
    first, second, normed, outgoing, received, answers, returned, hidden, total,
    counts, counts_in, placed_col,
    weight_sem, send_sem, recv_sem, ret_sem, count_sem,
):
    n = rows * cols
    tok_rows, width = tokens_ref.shape
    lanes = counts.shape[1]
    per = n // groups
    span = per * cap
    my_row, my_col = lax.axis_index("row"), lax.axis_index("col")
    me = my_row * cols + my_col

    def turn(step):
        if groups % 2:
            return step
        return lax.rem(step, 2) * (groups // 2) + lax.div(step, 2)

    def partner(place):
        q = n - 1 - place
        return (
            bit_xor(my_row, lax.rem(q, rows), rows),
            bit_xor(my_col, lax.div(q, rows), cols),
        )

    barrier = pltpu.get_barrier_semaphore()

    @pl.loop(0, n - 1)
    def _(place):
        pl.semaphore_signal(barrier, inc=1, device_id=partner(place), device_id_type=MESH)

    load_first = pltpu.make_async_copy(first_hbm.at[0], first, weight_sem.at[0])
    load_second = pltpu.make_async_copy(second_hbm.at[0], second, weight_sem.at[1])
    load_first.start()
    load_second.start()

    def slot_of(ids, within):
        offset = jnp.bitwise_xor(ids, me)
        q = (offset % cols) * rows + offset // cols
        return (n - 1 - q) * cap + within

    ids_row = ids_row_ref[...]
    at_row = lax.broadcasted_iota(jnp.int32, (tok_rows, tok_rows), 0)
    at_col = lax.broadcasted_iota(jnp.int32, (tok_rows, tok_rows), 1)
    hot_row = lax.broadcasted_iota(jnp.int32, (lanes, tok_rows), 0) == ids_row
    before = jnp.where(at_row < at_col, 1.0, 0.0).astype(jnp.bfloat16)
    earlier = jnp.dot(
        jnp.where(hot_row, 1.0, 0.0).astype(jnp.bfloat16), before, preferred_element_type=jnp.float32
    )
    within_row = jnp.sum(jnp.where(hot_row, earlier, 0.0), axis=0, keepdims=True)
    placed_row = slot_of(ids_row, within_row.astype(jnp.int32))

    wide = tokens_ref[...].astype(jnp.float32)
    scale = lax.rsqrt(jnp.mean(wide * wide, axis=1, keepdims=True) + 1e-06)
    normed[...] = (wide * scale * gain_ref[...]).astype(jnp.bfloat16)

    def as_blocks(values):
        return values.reshape(per, cap, width).astype(jnp.bfloat16)

    def as_rows(ref, g):
        blocks = ref[pl.ds(g * per, per)]
        if cap % 16 == 0:
            return blocks.reshape(span, width)
        return blocks.astype(jnp.float32).reshape(span, width).astype(jnp.bfloat16)

    def exchange(source, target, sem, out_sem, g):
        @pl.loop(0, per)
        def _(i):
            place = g * per + i

            @pl.when(place < n - 1)
            def _():
                pltpu.make_async_remote_copy(
                    src_ref=source.at[place],
                    dst_ref=target.at[place],
                    send_sem=out_sem,
                    recv_sem=sem.at[g],
                    device_id=partner(place),
                    device_id_type=MESH,
                ).start()

            @pl.when(place == n - 1)
            def _():
                pltpu.make_async_copy(source.at[n - 1], target.at[n - 1], sem.at[g]).start()

    def wait_group(target, sem, g):
        whole = target.at[pl.ds(g * per, per)]
        pltpu.make_async_copy(whole, whole, sem.at[g]).wait()

    @pl.loop(0, groups)
    def _(step):
        g = turn(step)
        slot = lax.broadcasted_iota(jnp.int32, (span, tok_rows), 0) + g * span
        table = jnp.where(slot == placed_row, 1.0, 0.0).astype(jnp.bfloat16)
        outgoing[pl.ds(g * per, per)] = as_blocks(
            jnp.dot(table, normed[...], preferred_element_type=jnp.float32)
        )

        @pl.when(step == 0)
        def _():
            pl.semaphore_wait(barrier, n - 1)

        exchange(outgoing, received, recv_sem, send_sem.at[0], g)

    counts[...] = lax.dot_general(
        jnp.ones((8, tok_rows), jnp.bfloat16),
        jnp.where(hot_row, 1.0, 0.0).astype(jnp.bfloat16),
        (((1,), (1,)), ((), ())),
        preferred_element_type=jnp.float32,
    )[0:1]
    turned = jnp.where(at_row == at_col, placed_row.astype(jnp.float32), 0.0)
    placed_col[...] = jnp.sum(turned, axis=1, keepdims=True).astype(jnp.int32)
    total[...] = jnp.zeros_like(total)

    @pl.loop(0, n - 1)
    def _(place):
        pltpu.make_async_remote_copy(
            src_ref=counts,
            dst_ref=counts_in.at[place],
            send_sem=send_sem.at[2],
            recv_sem=count_sem,
            device_id=partner(place),
            device_id_type=MESH,
        ).start()

    load_first.wait()
    load_second.wait()

    @pl.loop(0, groups)
    def _(step):
        g = turn(lax.rem(step + groups - 1, groups))
        wait_group(received, recv_sem, g)
        slab = as_rows(received, g)

        @pl.loop(0, first.shape[1] // ff_tile)
        def _(i):
            part = pl.ds(pl.multiple_of(i * ff_tile, ff_tile), ff_tile)
            grown = jnp.dot(slab, first[:, part], preferred_element_type=jnp.float32)
            hidden[:, part] = jnp.maximum(grown, 0.0).astype(jnp.bfloat16)

        @pl.loop(0, width // out_tile)
        def _(i):
            part = pl.ds(pl.multiple_of(i * out_tile, out_tile), out_tile)
            made = jnp.dot(hidden[...], second[:, part], preferred_element_type=jnp.float32)
            answers[pl.ds(g * per, per), :, part] = made.reshape(per, cap, out_tile).astype(
                jnp.bfloat16
            )

        exchange(answers, returned, ret_sem, send_sem.at[1], g)

    arrived = counts_in.at[pl.ds(0, n - 1)]
    pltpu.make_async_copy(arrived, arrived, count_sem).wait()
    sums = jnp.sum(counts_in[pl.ds(0, n - 1)], axis=0) + counts[...]
    mine = lax.broadcasted_iota(jnp.int32, (1, lanes), 1) == me
    routed_ref[0] = jnp.sum(jnp.where(mine, sums, 0.0)).astype(jnp.int32)

    @pl.loop(0, groups)
    def _(step):
        g = turn(lax.rem(step + groups - 1, groups))
        wait_group(returned, ret_sem, g)
        slot = lax.broadcasted_iota(jnp.int32, (tok_rows, span), 1) + g * span
        table = jnp.where(slot == placed_col[...], 1.0, 0.0).astype(jnp.bfloat16)
        total[...] += jnp.dot(table, as_rows(returned, g), preferred_element_type=jnp.float32)

    back_ref[...] = total[...].astype(jnp.bfloat16)

    sent = outgoing.at[pl.ds(0, n - 1)]
    pltpu.make_async_copy(sent, sent, send_sem.at[0]).wait()
    pltpu.make_async_copy(sent, sent, send_sem.at[1]).wait()
    pltpu.make_async_copy(arrived, arrived, send_sem.at[2]).wait()


def on_device(rows, cols, tokens, expert_ids, gate_prob, norm_gain, weight_in, weight_out):
    tok_rows, width = tokens.shape
    hidden_width = weight_in.shape[2]
    n = rows * cols
    cap = 2 * tok_rows // n
    lanes = -(-n // 128) * 128
    per = max(1, min(n, 256 // cap))
    groups = n // per
    vmem = pl.BlockSpec(memory_space=pltpu.VMEM)
    hbm = pl.BlockSpec(memory_space=pl.ANY)
    block = pltpu.VMEM((n, cap, width), jnp.bfloat16)
    back, routed = pl.pallas_call(
        functools.partial(kernel, rows, cols, cap, groups, min(512, hidden_width), min(256, width)),
        out_shape=(
            jax.ShapeDtypeStruct((tok_rows, width), jnp.bfloat16),
            jax.ShapeDtypeStruct((1,), jnp.int32),
        ),
        in_specs=[vmem, vmem, vmem, hbm, hbm],
        out_specs=(vmem, pl.BlockSpec(memory_space=pltpu.SMEM)),
        scratch_shapes=[
            pltpu.VMEM((width, hidden_width), jnp.bfloat16),
            pltpu.VMEM((hidden_width, width), jnp.bfloat16),
            pltpu.VMEM((tok_rows, width), jnp.bfloat16),
            block, block, block, block,
            pltpu.VMEM((per * cap, hidden_width), jnp.bfloat16),
            pltpu.VMEM((tok_rows, width), jnp.float32),
            pltpu.VMEM((1, lanes), jnp.float32),
            pltpu.VMEM((n, 1, lanes), jnp.float32),
            pltpu.VMEM((tok_rows, 1), jnp.int32),
            pltpu.SemaphoreType.DMA((2,)),
            pltpu.SemaphoreType.DMA((3,)),
            pltpu.SemaphoreType.DMA((groups,)),
            pltpu.SemaphoreType.DMA((groups,)),
            pltpu.SemaphoreType.DMA,
        ],
        compiler_params=pltpu.CompilerParams(
            collective_id=0, has_side_effects=True, vmem_limit_bytes=56 * 1024 * 1024
        ),
    )(
        tokens,
        expert_ids.reshape(1, tok_rows),
        norm_gain.reshape(1, width),
        weight_in,
        weight_out,
    )
    wide = tokens.astype(jnp.float32)
    mixed = (wide + gate_prob[:, None] * back.astype(jnp.float32)).astype(jnp.bfloat16)
    return (mixed, routed)


def solution(mesh):
    return jax.shard_map(
        functools.partial(on_device, mesh.shape["row"], mesh.shape["col"]),
        mesh=mesh,
        in_specs=(
            P(("row", "col"), None),
            P(("row", "col"), None),
            P(("row", "col")),
            P(),
            P(("row", "col"), None, None),
            P(("row", "col"), None, None),
        ),
        out_specs=(P(("row", "col"), None), P(("row", "col"))),
        check_vma=False,
    )
```

profile of v0, /device:TPU:0, one launch (start us, length us, event | category | flops | bytes accessed | tf_op | source)
XLA Modules:
  0.0 111.5 jit_solution(132514263278800078)
XLA Ops:
  0.6 0.0 copy-start
  0.6 0.0 copy-start.1
  0.7 106.5 %shard_map.77 = (bf16[512,1024]{1,0:T(8,128)(2,1)}, s32[1]{0:T(128)}) custom-call(bf16[512,1024]{1,0:T(8,128)(2,1)} %tokens_ref.1, s32[1,512]{1,0:T(1,128)} %bitcast.3, f32[1,1024]{1,0:T(1,128)} %bitcast.2, bf16[1,1024,4096]{2,1,0:T(8,128)(2,1)} %first_hbm.1, bf16[1,4096,1024]{2,1,0:T(8,128)(2,1)} %second_hbm.1), custom_call_target="tpu_custom_call" | custom-call | tf_op jit(solution)/shard_map/pallas_call | solution.py:207
  107.1 0.0 copy-done
  107.1 0.0 copy-done.1
  107.1 2.6 %add_convert_fusion = bf16[512,1024]{1,0:T(8,128)(2,1)} fusion(bf16[512,1024]{1,0:T(8,128)(2,1)} %get-tuple-element.4, bf16[512,1024]{1,0:T(8,128)(2,1)S(1)} %copy-done, f32[512]{0:T(512)S(1)} %copy-done.1), kind=kLoop, calls=%fused_computation | loop fusion | flops 2621440 | bytes 3147776 | tf_op jit(solution)/shard_map/convert_element_type | solution.py:242
Async XLA Ops:
  0.6 106.5 %copy-start = (bf16[512,1024]{1,0:T(8,128)(2,1)S(1)}, bf16[512,1024]{1,0:T(8,128)(2,1)}, u32[]{:S(2)}) copy-start(bf16[512,1024]{1,0:T(8,128)(2,1)} %tokens_ref.1) | copy-start | bytes 3145732
  0.6 106.5 %copy-start.1 = (f32[512]{0:T(512)S(1)}, f32[512]{0:T(512)}, u32[]{:S(2)}) copy-start(f32[512]{0:T(512)} %param.8) | copy-start | bytes 6148
where the time goes:
time: 112 us; the launch traced here: 111 us
  Pallas kernels  106 us (95%)
  other arithmetic  2.57 us (2%)
  between operations  2.43 us (2%)
    pallas_call x1, Pallas kernels, on_device(): pl.pallas_call(functools.partial(kernel, rows, cols, cap, groups, min(512...  106 us
    convert_element_type x1, other arithmetic, on_device(): (wide + gate_prob[:, None] * back.astype(jnp.float32)).astype(jnp.bfloat16)  2.57 us

commit v1 on v0

--- a/solution.py
+++ b/solution.py
@@ -193,7 +193,334 @@
     pltpu.make_async_copy(arrived, arrived, send_sem.at[2]).wait()
 
 
-def on_device(rows, cols, tokens, expert_ids, gate_prob, norm_gain, weight_in, weight_out):
+def flipped(a, mask, size):
+    out, unit = 0, 1
+    while unit < size:
+        bit = lax.rem(lax.div(a, unit), 2)
+        out = out + ((1 - bit) if (mask // unit) % 2 else bit) * unit
+        unit *= 2
+    return out
+
+
+def packed_kernel(
+    rows, cols, low, cap, keep, parts, ff_tile, out_tile,
+    tokens_ref, ids_row_ref, gate_row_ref, gain_ref, first_hbm, second_hbm,
+    mixed_ref, routed_ref, over_ref,
+    first, second, normed, packed, packed_in, slots, slots_in, answers, answers_in,
+    back, back_in, hidden, total, counts, counts_far, counts_in,
+    index_row, index_col, placed_col, gate_col,
+    weight_sem, send_sem, far_sem, near_sem, answer_sem, back_sem, count_sem,
+):
+    n = rows * cols
+    planes = cols // low
+    per = n // planes
+    span = per * cap
+    tok_rows, width = tokens_ref.shape
+    wide_part = width // parts
+    lanes = counts.shape[1]
+    my_row, my_col = lax.axis_index("row"), lax.axis_index("col")
+    me = my_row * cols + my_col
+    row_at = [flipped(my_row, c, rows) for c in range(rows)]
+    low_at = [flipped(lax.rem(my_col, low), c, low) for c in range(low)]
+    plane_at = [flipped(lax.div(my_col, low), c, planes) * low for c in range(planes)]
+    far = list(range(planes - 1, 0, -1))
+
+    def device(k, j):
+        return (row_at[j % rows], plane_at[k] + low_at[j // rows])
+
+    def send(source, target, out_sem, sem, where):
+        pltpu.make_async_remote_copy(
+            src_ref=source, dst_ref=target, send_sem=out_sem, recv_sem=sem,
+            device_id=where, device_id_type=MESH,
+        ).start()
+
+    def wait(ref, sem):
+        pltpu.make_async_copy(ref, ref, sem).wait()
+
+    barrier = pltpu.get_barrier_semaphore()
+    for k in range(planes):
+        for j in range(per):
+            if k or j:
+                pl.semaphore_signal(barrier, inc=1, device_id=device(k, j), device_id_type=MESH)
+
+    load_first = pltpu.make_async_copy(first_hbm.at[0], first, weight_sem.at[0])
+    load_second = pltpu.make_async_copy(second_hbm.at[0], second, weight_sem.at[1])
+    load_first.start()
+    load_second.start()
+
+    def place_of(ids):
+        offset = jnp.bitwise_xor(ids, me)
+        return (offset % cols) // low, offset // cols + rows * (offset % low)
+
+    def ones_at(condition):
+        return jnp.where(condition, 1.0, 0.0).astype(jnp.bfloat16)
+
+    ids_row = ids_row_ref[...]
+    at_row = lax.broadcasted_iota(jnp.int32, (tok_rows, tok_rows), 0)
+    at_col = lax.broadcasted_iota(jnp.int32, (tok_rows, tok_rows), 1)
+    hot = lax.broadcasted_iota(jnp.int32, (lanes, tok_rows), 0) == ids_row
+    hot_bf = ones_at(hot)
+    earlier = jnp.dot(hot_bf, ones_at(at_row < at_col), preferred_element_type=jnp.float32)
+    within = jnp.sum(jnp.where(hot, earlier, 0.0), axis=0, keepdims=True)
+    plane_e, near_e = place_of(lax.broadcasted_iota(jnp.int32, (lanes, 1), 0))
+    plane_t, near_t = place_of(ids_row)
+    count_e = jnp.sum(jnp.where(hot, 1.0, 0.0), axis=1, keepdims=True)
+    sooner = (plane_e == plane_t) & (near_e < near_t)
+    ahead = jnp.sum(jnp.where(sooner, count_e, 0.0), axis=0, keepdims=True)
+    start = jnp.where(plane_t == 0, near_t * cap, ahead.astype(jnp.int32))
+    placed_row = plane_t * span + start + within.astype(jnp.int32)
+
+    wide = tokens_ref[...].astype(jnp.float32)
+    scale = lax.rsqrt(jnp.mean(wide * wide, axis=1, keepdims=True) + 1e-06)
+    normed[...] = (wide * scale * gain_ref[...]).astype(jnp.bfloat16)
+
+    tally = lax.dot_general(
+        jnp.ones((8, tok_rows), jnp.bfloat16), hot_bf,
+        (((1,), (1,)), ((), ())), preferred_element_type=jnp.float32,
+    )[0:1]
+    lane = lax.broadcasted_iota(jnp.int32, (1, lanes), 1)
+    plane_l, _ = place_of(lane)
+    over = jnp.zeros((1, 1), jnp.float32)
+    for k in far:
+        held = jnp.sum(jnp.where(plane_l == k, tally, 0.0), axis=1, keepdims=True)
+        over = over + jnp.where(held > keep, 1.0, 0.0)
+    counts[...] = tally + jnp.where(lane == n, over, 0.0)
+
+    def columns(h):
+        return pl.ds(h * wide_part, wide_part)
+
+    def gather_from(k, size):
+        slot = lax.broadcasted_iota(jnp.int32, (size, tok_rows), 0) + k * span
+        return ones_at(slot == placed_row)
+
+    def pack(k):
+        table = gather_from(k, keep)
+        for h in range(parts):
+            packed[k, h] = jnp.dot(
+                table, normed[:, columns(h)], preferred_element_type=jnp.float32
+            ).astype(jnp.bfloat16)
+
+    def send_far(k):
+        for h in range(parts):
+            send(packed.at[k, h], packed_in.at[k, h], send_sem.at[0], far_sem.at[k, h], device(k, 0))
+
+    def send_near(source, target, out_sem, sem, k, h):
+        for j in range(1, per):
+            block = pl.ds(j * cap, cap)
+            send(
+                source.at[k, h, block], target.at[k, h, block], out_sem, sem.at[k, h], device(0, j)
+            )
+
+    def wait_near(target, sem, k, h):
+        wait(target.at[k, h, pl.ds(cap, span - cap)], sem.at[k, h])
+
+    def fill(k, h, values):
+        made = values.astype(jnp.bfloat16)
+        slots_in[k, h, 0:cap] = made[0:cap]
+        slots[k, h] = made
+        send_near(slots, slots_in, send_sem.at[1], near_sem, k, h)
+
+    pack(far[0])
+    pl.semaphore_wait(barrier, n - 1)
+    for k in far:
+        send(counts, counts_far.at[k], send_sem.at[4], count_sem.at[0], device(k, 0))
+    send_far(far[0])
+    table = gather_from(0, span)
+    for h in range(parts):
+        fill(0, h, jnp.dot(table, normed[:, columns(h)], preferred_element_type=jnp.float32))
+    for k in far[1:]:
+        pack(k)
+        send_far(k)
+    for k in range(planes):
+        for j in range(1, per):
+            send(
+                counts, counts_in.at[k * (per - 1) + j - 1], send_sem.at[5], count_sem.at[1],
+                device(k, j),
+            )
+
+    def to_column(row, size):
+        there = lax.broadcasted_iota(jnp.int32, (size, size), 0)
+        here = lax.broadcasted_iota(jnp.int32, (size, size), 1)
+        return jnp.sum(jnp.where(there == here, row, 0.0), axis=1, keepdims=True)
+
+    placed_col[...] = to_column(placed_row.astype(jnp.float32), tok_rows).astype(jnp.int32)
+    gate_col[...] = to_column(gate_row_ref[...], tok_rows)
+
+    wait(counts_far.at[pl.ds(1, planes - 1)], count_sem.at[0])
+    expert = lax.broadcasted_iota(jnp.int32, (lanes, span), 0)
+    plane_s, near_s = place_of(expert)
+    here = (plane_s == 0) & (expert < n)
+    slot = lax.broadcasted_iota(jnp.int32, (lanes, span), 1)
+    at_block = ones_at(here & (near_s == slot // cap))
+    before_block = ones_at(here & (near_s < slot // cap))
+    slot_row = lax.broadcasted_iota(jnp.int32, (1, span), 1)
+    rank = (slot_row % cap).astype(jnp.float32)
+    for k in far:
+        tall = jnp.broadcast_to(counts_far[k], (8, lanes)).astype(jnp.bfloat16)
+        held = jnp.dot(tall, at_block, preferred_element_type=jnp.float32)[0:1]
+        begin = jnp.dot(tall, before_block, preferred_element_type=jnp.float32)[0:1]
+        index = jnp.where(rank < held, begin + rank, -1.0)
+        index_row[k] = index.astype(jnp.int32)
+        index_col[k] = to_column(index, span).astype(jnp.int32)
+
+    load_first.wait()
+    load_second.wait()
+
+    def relay(k, h):
+        wait(packed_in.at[k, h], far_sem.at[k, h])
+        slot = lax.broadcasted_iota(jnp.int32, (span, keep), 1)
+        table = ones_at(slot == index_col[k])
+        fill(k, h, jnp.dot(table, packed_in[k, h], preferred_element_type=jnp.float32))
+
+    def expert_step(k):
+        for h in range(parts):
+            wait_near(slots_in, near_sem, k, h)
+
+        @pl.loop(0, first.shape[1] // ff_tile)
+        def _(i):
+            part = pl.ds(pl.multiple_of(i * ff_tile, ff_tile), ff_tile)
+            grown = jnp.dot(slots_in[k, 0], first[columns(0), part], preferred_element_type=jnp.float32)
+            for h in range(1, parts):
+                grown += jnp.dot(
+                    slots_in[k, h], first[columns(h), part], preferred_element_type=jnp.float32
+                )
+            hidden[:, part] = jnp.maximum(grown, 0.0).astype(jnp.bfloat16)
+
+        for h in range(parts):
+
+            @pl.loop(0, wide_part // out_tile)
+            def _(i):
+                at = pl.multiple_of(i * out_tile, out_tile)
+                part = pl.ds(pl.multiple_of(h * wide_part + i * out_tile, out_tile), out_tile)
+                made = jnp.dot(hidden[...], second[:, part], preferred_element_type=jnp.float32)
+                made = made.astype(jnp.bfloat16)
+                answers[k, h, :, pl.ds(at, out_tile)] = made
+                answers_in[k, h, 0:cap, pl.ds(at, out_tile)] = made[0:cap]
+
+            send_near(answers, answers_in, send_sem.at[2], answer_sem, k, h)
+
+    def give_back(k, h):
+        wait_near(answers_in, answer_sem, k, h)
+        slot = lax.broadcasted_iota(jnp.int32, (keep, span), 0)
+        table = ones_at(slot == index_row[k])
+        back[k, h] = jnp.dot(
+            table, answers_in[k, h], preferred_element_type=jnp.float32
+        ).astype(jnp.bfloat16)
+        send(back.at[k, h], back_in.at[k, h], send_sem.at[3], back_sem.at[k, h], device(k, 0))
+
+    def picked(k, h):
+        size = keep if k else span
+        if k:
+            wait(back_in.at[k, h], back_sem.at[k, h])
+        else:
+            wait_near(answers_in, answer_sem, 0, h)
+        source = back_in if k else answers_in
+        slot = lax.broadcasted_iota(jnp.int32, (tok_rows, size), 1) + k * span
+        table = ones_at(slot == placed_col[...])
+        return jnp.dot(table, source[k, h], preferred_element_type=jnp.float32)
+
+    expert_step(0)
+    for h in range(parts):
+        relay(far[0], h)
+    for i, k in enumerate(far):
+        expert_step(k)
+        later = far[i + 1] if i + 1 < len(far) else None
+        if later is not None:
+            relay(later, 0)
+        for h in range(parts):
+            give_back(k, h)
+        if later is not None:
+            for h in range(1, parts):
+                relay(later, h)
+
+    wait(counts_in, count_sem.at[1])
+    sums = jnp.sum(counts_in[...], axis=0) + counts[...]
+    sums += jnp.sum(counts_far[pl.ds(1, planes - 1)], axis=0)
+    routed_ref[0] = jnp.sum(jnp.where(lane == me, sums, 0.0)).astype(jnp.int32)
+    over_ref[0] = jnp.sum(jnp.where(lane == n, sums, 0.0)).astype(jnp.int32)
+
+    for h in range(parts):
+        total[h] = picked(0, h)
+    for k in far[:-1]:
+        for h in range(parts):
+            total[h] += picked(k, h)
+    for h in range(parts):
+        found = total[h] + picked(far[-1], h)
+        kept = tokens_ref[:, columns(h)].astype(jnp.float32)
+        mixed_ref[:, columns(h)] = (kept + gate_col[...] * found).astype(jnp.bfloat16)
+
+    wait(packed.at[pl.ds(1, planes - 1)], send_sem.at[0])
+    wait(slots.at[:, :, pl.ds(cap, span - cap)], send_sem.at[1])
+    wait(answers.at[:, :, pl.ds(cap, span - cap)], send_sem.at[2])
+    wait(back.at[pl.ds(1, planes - 1)], send_sem.at[3])
+    wait(counts_far.at[pl.ds(1, planes - 1)], send_sem.at[4])
+    wait(counts_in, send_sem.at[5])
+
+
+def packed_layer(rows, cols, tokens, expert_ids, gate_prob, norm_gain, weight_in, weight_out):
+    tok_rows, width = tokens.shape
+    hidden_width = weight_in.shape[2]
+    n = rows * cols
+    low = min(2, cols)
+    planes = cols // low
+    per = n // planes
+    cap = 2 * tok_rows // n
+    span = per * cap
+    keep = 3 * span // 4
+    parts = 2
+    part = width // parts
+    lanes = -(-(n + 1) // 128) * 128
+    vmem = pl.BlockSpec(memory_space=pltpu.VMEM)
+    smem = pl.BlockSpec(memory_space=pltpu.SMEM)
+    hbm = pl.BlockSpec(memory_space=pl.ANY)
+    tight = pltpu.VMEM((planes, parts, keep, part), jnp.bfloat16)
+    loose = pltpu.VMEM((planes, parts, span, part), jnp.bfloat16)
+    each = pltpu.SemaphoreType.DMA((planes, parts))
+    return pl.pallas_call(
+        functools.partial(
+            packed_kernel, rows, cols, low, cap, keep, parts,
+            min(512, hidden_width), min(256, part),
+        ),
+        out_shape=(
+            jax.ShapeDtypeStruct((tok_rows, width), jnp.bfloat16),
+            jax.ShapeDtypeStruct((1,), jnp.int32),
+            jax.ShapeDtypeStruct((1,), jnp.int32),
+        ),
+        in_specs=[vmem, vmem, vmem, vmem, hbm, hbm],
+        out_specs=(vmem, smem, smem),
+        scratch_shapes=[
+            pltpu.VMEM((width, hidden_width), jnp.bfloat16),
+            pltpu.VMEM((hidden_width, width), jnp.bfloat16),
+            pltpu.VMEM((tok_rows, width), jnp.bfloat16),
+            tight, tight, loose, loose, loose, loose, tight, tight,
+            pltpu.VMEM((span, hidden_width), jnp.bfloat16),
+            pltpu.VMEM((parts, tok_rows, part), jnp.float32),
+            pltpu.VMEM((1, lanes), jnp.float32),
+            pltpu.VMEM((planes, 1, lanes), jnp.float32),
+            pltpu.VMEM((planes * (per - 1), 1, lanes), jnp.float32),
+            pltpu.VMEM((planes, 1, span), jnp.int32),
+            pltpu.VMEM((planes, span, 1), jnp.int32),
+            pltpu.VMEM((tok_rows, 1), jnp.int32),
+            pltpu.VMEM((tok_rows, 1), jnp.float32),
+            pltpu.SemaphoreType.DMA((2,)),
+            pltpu.SemaphoreType.DMA((6,)),
+            each, each, each, each,
+            pltpu.SemaphoreType.DMA((2,)),
+        ],
+        compiler_params=pltpu.CompilerParams(
+            collective_id=0, has_side_effects=True, vmem_limit_bytes=56 * 1024 * 1024
+        ),
+    )(
+        tokens,
+        expert_ids.reshape(1, tok_rows),
+        gate_prob.reshape(1, tok_rows),
+        norm_gain.reshape(1, width),
+        weight_in,
+        weight_out,
+    )
+
+
+def slotted_layer(rows, cols, tokens, expert_ids, gate_prob, norm_gain, weight_in, weight_out):
     tok_rows, width = tokens.shape
     hidden_width = weight_in.shape[2]
     n = rows * cols
@@ -229,7 +556,7 @@
             pltpu.SemaphoreType.DMA,
         ],
         compiler_params=pltpu.CompilerParams(
-            collective_id=0, has_side_effects=True, vmem_limit_bytes=56 * 1024 * 1024
+            collective_id=1, has_side_effects=True, vmem_limit_bytes=56 * 1024 * 1024
         ),
     )(
         tokens,
@@ -240,6 +567,15 @@
     )
     wide = tokens.astype(jnp.float32)
     mixed = (wide + gate_prob[:, None] * back.astype(jnp.float32)).astype(jnp.bfloat16)
+    return mixed
+
+
+def on_device(rows, cols, *args):
+    mixed, routed, over = packed_layer(rows, cols, *args)
+    mixed = lax.cond(
+        over[0] > 0, lambda given, *all_args: slotted_layer(rows, cols, *all_args),
+        lambda given, *all_args: given, mixed, *args,
+    )
     return (mixed, routed)
 
 

time: 112 us -> 105 us (0.938)
  Pallas kernels: 106 us -> 101 us
  other arithmetic: 2.57 us -> 0 us
    pallas_call x1, Pallas kernels: 106 us -> 101 us  [packed_layer(): pl.pallas_call(functools.partial(packed_kernel, rows, cols, low, cap, kee...]
    convert_element_type x1 -> x0, other arithmetic: 2.57 us -> none  [on_device(): (wide + gate_prob[:, None] * back.astype(jnp.float32)).astype(jnp.bfloat16)]
where the time goes in v1:
time: 105 us
  Pallas kernels  101 us (96%)
  between operations  3.02 us (3%)
    pallas_call x1, Pallas kernels, packed_layer(): pl.pallas_call(functools.partial(packed_kernel, rows, cols, low, cap, kee...  101 us

profile of v1, /device:TPU:0, one launch (start us, length us, event | category | flops | bytes accessed | tf_op | source)
XLA Modules:
  0.0 104.7 jit_solution(17184009381851282855)
XLA Ops:
  0.6 0.0 copy-start
  0.6 0.0 copy-start.1
  0.6 0.0 copy-start.2
  0.7 0.0 copy-start.3
  0.7 100.6 %shard_map.77 = (bf16[512,1024]{1,0:T(8,128)(2,1)S(1)}, s32[1]{0:T(128)}, s32[1]{0:T(128)}) custom-call(bf16[512,1024]{1,0:T(8,128)(2,1)} %tokens_ref.1, s32[1,512]{1,0:T(1,128)} %bitcast.9, f32[1,512]{1,0:T(1,128)} %bitcast.8, f32[1,1024]{1,0:T(1,128)} %bitcast.6, bf16[1,1024,4096]{2,1,0:T(8,128)(2,1)} %first_hbm.1, bf16[1,4096,1024]{2,1,0:T(8,128)(2,1)} %second_hbm.1), custom_call_target="tpu_custom_call" | custom-call | tf_op jit(solution)/shard_map/pallas_call | solution.py:479
  101.8 0.0 copy-done
  101.8 0.0 copy-done.1
  101.8 0.0 copy-done.2
  101.8 0.0 copy-done.3
  101.8 0.2 conditional.1
  102.0 1.0 copy.12
Async XLA Ops:
  0.6 101.2 %copy-start = (bf16[512,1024]{1,0:T(8,128)(2,1)S(1)}, bf16[512,1024]{1,0:T(8,128)(2,1)}, u32[]{:S(2)}) copy-start(bf16[512,1024]{1,0:T(8,128)(2,1)} %tokens_ref.1) | copy-start | bytes 3145732
  0.6 101.2 %copy-start.1 = (f32[1024]{0:T(1024)S(1)}, f32[1024]{0:T(1024)}, u32[]{:S(2)}) copy-start(f32[1024]{0:T(1024)} %param.11) | copy-start | bytes 12292
  0.6 101.2 %copy-start.2 = (f32[512]{0:T(512)S(1)}, f32[512]{0:T(512)}, u32[]{:S(2)}) copy-start(f32[512]{0:T(512)} %param.10) | copy-start | bytes 6148
  0.7 101.2 %copy-start.3 = (s32[512,1]{0,1:T(1,128)S(1)}, s32[512,1]{0,1:T(1,128)}, u32[]{:S(2)}) copy-start(s32[512,1]{0,1:T(1,128)} %param.9) | copy-start | bytes 6148

commit v2 on v1

--- a/solution.py
+++ b/solution.py
@@ -224,6 +224,10 @@
     low_at = [flipped(lax.rem(my_col, low), c, low) for c in range(low)]
     plane_at = [flipped(lax.div(my_col, low), c, planes) * low for c in range(planes)]
     far = list(range(planes - 1, 0, -1))
+    half = planes // 2
+    sent = [planes - 1 - k for i in range(half) for k in (i, i + half)][: planes - 1]
+    if planes % 2:
+        sent = far
 
     def device(k, j):
         return (row_at[j % rows], plane_at[k] + low_at[j // rows])
@@ -234,8 +238,9 @@
             device_id=where, device_id_type=MESH,
         ).start()
 
-    def wait(ref, sem):
-        pltpu.make_async_copy(ref, ref, sem).wait()
+    def wait(ref, sem, name="wait_last"):
+        with jax.named_scope(name):
+            pltpu.make_async_copy(ref, ref, sem).wait()
 
     barrier = pltpu.get_barrier_semaphore()
     for k in range(planes):
@@ -311,8 +316,8 @@
                 source.at[k, h, block], target.at[k, h, block], out_sem, sem.at[k, h], device(0, j)
             )
 
-    def wait_near(target, sem, k, h):
-        wait(target.at[k, h, pl.ds(cap, span - cap)], sem.at[k, h])
+    def wait_near(target, sem, k, h, name):
+        wait(target.at[k, h, pl.ds(cap, span - cap)], sem.at[k, h], f"{name}#k={k}#h={h}")
 
     def fill(k, h, values):
         made = values.astype(jnp.bfloat16)
@@ -321,14 +326,15 @@
         send_near(slots, slots_in, send_sem.at[1], near_sem, k, h)
 
     pack(far[0])
-    pl.semaphore_wait(barrier, n - 1)
+    with jax.named_scope("barrier_wait"):
+        pl.semaphore_wait(barrier, n - 1)
     for k in far:
         send(counts, counts_far.at[k], send_sem.at[4], count_sem.at[0], device(k, 0))
     send_far(far[0])
     table = gather_from(0, span)
     for h in range(parts):
         fill(0, h, jnp.dot(table, normed[:, columns(h)], preferred_element_type=jnp.float32))
-    for k in far[1:]:
+    for k in sent[1:]:
         pack(k)
         send_far(k)
     for k in range(planes):
@@ -346,7 +352,7 @@
     placed_col[...] = to_column(placed_row.astype(jnp.float32), tok_rows).astype(jnp.int32)
     gate_col[...] = to_column(gate_row_ref[...], tok_rows)
 
-    wait(counts_far.at[pl.ds(1, planes - 1)], count_sem.at[0])
+    wait(counts_far.at[pl.ds(1, planes - 1)], count_sem.at[0], "wait_counts")
     expert = lax.broadcasted_iota(jnp.int32, (lanes, span), 0)
     plane_s, near_s = place_of(expert)
     here = (plane_s == 0) & (expert < n)
@@ -363,18 +369,19 @@
         index_row[k] = index.astype(jnp.int32)
         index_col[k] = to_column(index, span).astype(jnp.int32)
 
-    load_first.wait()
-    load_second.wait()
+    with jax.named_scope("wait_weights"):
+        load_first.wait()
+        load_second.wait()
 
     def relay(k, h):
-        wait(packed_in.at[k, h], far_sem.at[k, h])
+        wait(packed_in.at[k, h], far_sem.at[k, h], f"wait_far#k={k}#h={h}")
         slot = lax.broadcasted_iota(jnp.int32, (span, keep), 1)
         table = ones_at(slot == index_col[k])
         fill(k, h, jnp.dot(table, packed_in[k, h], preferred_element_type=jnp.float32))
 
-    def expert_step(k):
+    def grow(k):
         for h in range(parts):
-            wait_near(slots_in, near_sem, k, h)
+            wait_near(slots_in, near_sem, k, h, "wait_slots")
 
         @pl.loop(0, first.shape[1] // ff_tile)
         def _(i):
@@ -386,21 +393,21 @@
                 )
             hidden[:, part] = jnp.maximum(grown, 0.0).astype(jnp.bfloat16)
 
-        for h in range(parts):
-
-            @pl.loop(0, wide_part // out_tile)
-            def _(i):
-                at = pl.multiple_of(i * out_tile, out_tile)
-                part = pl.ds(pl.multiple_of(h * wide_part + i * out_tile, out_tile), out_tile)
-                made = jnp.dot(hidden[...], second[:, part], preferred_element_type=jnp.float32)
-                made = made.astype(jnp.bfloat16)
-                answers[k, h, :, pl.ds(at, out_tile)] = made
-                answers_in[k, h, 0:cap, pl.ds(at, out_tile)] = made[0:cap]
-
-            send_near(answers, answers_in, send_sem.at[2], answer_sem, k, h)
+    def shrink(k, h):
+        @pl.loop(0, wide_part // out_tile)
+        def _(i):
+            at = pl.multiple_of(i * out_tile, out_tile)
+            part = pl.ds(pl.multiple_of(h * wide_part + i * out_tile, out_tile), out_tile)
+            made = jnp.dot(hidden[...], second[:, part], preferred_element_type=jnp.float32)
+            made = made.astype(jnp.bfloat16)
+            answers[k, h, :, pl.ds(at, out_tile)] = made
+            answers_in[k, h, 0:cap, pl.ds(at, out_tile)] = made[0:cap]
+
+    def send_answers(k, h):
+        send_near(answers, answers_in, send_sem.at[2], answer_sem, k, h)
 
     def give_back(k, h):
-        wait_near(answers_in, answer_sem, k, h)
+        wait_near(answers_in, answer_sem, k, h, "wait_answers")
         slot = lax.broadcasted_iota(jnp.int32, (keep, span), 0)
         table = ones_at(slot == index_row[k])
         back[k, h] = jnp.dot(
@@ -411,27 +418,42 @@
     def picked(k, h):
         size = keep if k else span
         if k:
-            wait(back_in.at[k, h], back_sem.at[k, h])
+            wait(back_in.at[k, h], back_sem.at[k, h], f"wait_back#k={k}#h={h}")
         else:
-            wait_near(answers_in, answer_sem, 0, h)
+            wait_near(answers_in, answer_sem, 0, h, "wait_answers")
         source = back_in if k else answers_in
         slot = lax.broadcasted_iota(jnp.int32, (tok_rows, size), 1) + k * span
         table = ones_at(slot == placed_col[...])
         return jnp.dot(table, source[k, h], preferred_element_type=jnp.float32)
 
-    expert_step(0)
-    for h in range(parts):
+    halves = range(parts)
+    grow(0)
+    for h in halves:
+        shrink(0, h)
+    for h in halves:
         relay(far[0], h)
-    for i, k in enumerate(far):
-        expert_step(k)
-        later = far[i + 1] if i + 1 < len(far) else None
-        if later is not None:
-            relay(later, 0)
-        for h in range(parts):
-            give_back(k, h)
-        if later is not None:
+    todo = far[:1] + far[:0:-1]
+    for i, k in enumerate(todo):
+        grow(k)
+        after = todo[i + 1] if i + 1 < len(todo) else None
+        last = i + 2 == len(todo)
+        if after is not None:
+            relay(after, 0)
+            if last:
+                give_back(todo[i - 1], 0)
+                for h in range(1, parts):
+                    give_back(todo[i - 1], h)
             for h in range(1, parts):
-                relay(later, h)
+                relay(after, h)
+        for h in halves:
+            if after is None and i:
+                give_back(todo[i - 1], h)
+            shrink(k, h)
+            send_answers(k, h)
+    for h in halves:
+        send_answers(0, h)
+    for h in halves:
+        give_back(todo[-1], h)
 
     wait(counts_in, count_sem.at[1])
     sums = jnp.sum(counts_in[...], axis=0) + counts[...]
@@ -441,11 +463,11 @@
 
     for h in range(parts):
         total[h] = picked(0, h)
-    for k in far[:-1]:
+    for k in todo[:-1]:
         for h in range(parts):
             total[h] += picked(k, h)
     for h in range(parts):
-        found = total[h] + picked(far[-1], h)
+        found = total[h] + picked(todo[-1], h)
         kept = tokens_ref[:, columns(h)].astype(jnp.float32)
         mixed_ref[:, columns(h)] = (kept + gate_col[...] * found).astype(jnp.bfloat16)
 

time: 105 us -> 91.5 us (0.87)
  Pallas kernels: 101 us -> 87.1 us
    pallas_call x1, Pallas kernels: 101 us -> 87.1 us  [packed_layer(): pl.pallas_call(functools.partial(packed_kernel, rows, cols, low, cap, kee...]
where the time goes in v2:
time: 91.5 us; the launch traced here: 91.3 us
  Pallas kernels  87.1 us (95%)
  between operations  3.02 us (3%)
  local copies, waits for them, and re-layouts  0.99 us (1%)
    pallas_call x1, Pallas kernels, packed_layer(): pl.pallas_call(functools.partial(packed_kernel, rows, cols, low, cap, kee...  87.1 us

profile of v2, /device:TPU:0, one launch (start us, length us, event | category | flops | bytes accessed | tf_op | source)
XLA Modules:
  0.0 91.3 jit_solution(11748698259069930141)
XLA Ops:
  0.6 0.0 copy-start
  0.6 0.0 copy-start.1
  0.6 0.0 copy-start.2
  0.7 0.0 copy-start.3
  0.7 87.1 %shard_map.77 = (bf16[512,1024]{1,0:T(8,128)(2,1)S(1)}, s32[1]{0:T(128)}, s32[1]{0:T(128)}) custom-call(bf16[512,1024]{1,0:T(8,128)(2,1)} %tokens_ref.1, s32[1,512]{1,0:T(1,128)} %bitcast.9, f32[1,512]{1,0:T(1,128)} %bitcast.8, f32[1,1024]{1,0:T(1,128)} %bitcast.6, bf16[1,1024,4096]{2,1,0:T(8,128)(2,1)} %first_hbm.1, bf16[1,4096,1024]{2,1,0:T(8,128)(2,1)} %second_hbm.1), custom_call_target="tpu_custom_call" | custom-call | tf_op jit(solution)/shard_map/pallas_call | solution.py:501
  88.3 0.0 copy-done
  88.3 0.0 copy-done.1
  88.4 0.0 copy-done.2
  88.4 0.0 copy-done.3
  88.4 0.2 conditional.1
  88.6 1.0 %copy.12 = bf16[512,1024]{1,0:T(8,128)(2,1)} copy(bf16[512,1024]{1,0:T(8,128)(2,1)S(1)} %get-tuple-element.35) | data formatting | bytes 2097152
Async XLA Ops:
  0.6 87.7 %copy-start = (bf16[512,1024]{1,0:T(8,128)(2,1)S(1)}, bf16[512,1024]{1,0:T(8,128)(2,1)}, u32[]{:S(2)}) copy-start(bf16[512,1024]{1,0:T(8,128)(2,1)} %tokens_ref.1) | copy-start | bytes 3145732
  0.6 87.7 %copy-start.1 = (f32[1024]{0:T(1024)S(1)}, f32[1024]{0:T(1024)}, u32[]{:S(2)}) copy-start(f32[1024]{0:T(1024)} %param.11) | copy-start | bytes 12292
  0.6 87.7 %copy-start.2 = (f32[512]{0:T(512)S(1)}, f32[512]{0:T(512)}, u32[]{:S(2)}) copy-start(f32[512]{0:T(512)} %param.10) | copy-start | bytes 6148
  0.7 87.7 %copy-start.3 = (s32[512,1]{0,1:T(1,128)S(1)}, s32[512,1]{0,1:T(1,128)}, u32[]{:S(2)}) copy-start(s32[512,1]{0,1:T(1,128)} %param.9) | copy-start | bytes 6148

commit v3 on v2

--- a/solution.py
+++ b/solution.py
@@ -204,12 +204,12 @@
 
 def packed_kernel(
     rows, cols, low, cap, keep, parts, ff_tile, out_tile,
-    tokens_ref, ids_row_ref, gate_row_ref, gain_ref, first_hbm, second_hbm,
-    mixed_ref, routed_ref, over_ref,
-    first, second, normed, packed, packed_in, slots, slots_in, answers, answers_in,
-    back, back_in, hidden, total, counts, counts_far, counts_in,
+    tokens_hbm, ids_hbm, gate_hbm, gain_hbm, first_hbm, second_hbm,
+    mixed_hbm, routed_ref, over_ref,
+    tokens_ref, ids_row_ref, gate_row_ref, gain_ref, mixed_ref, first, second, normed, packed, packed_in, slots, slots_in, answers, answers_in,
+    back, back_in, hidden, total, counts, counts_far, sums, sums_in,
     index_row, index_col, placed_col, gate_col,
-    weight_sem, send_sem, far_sem, near_sem, answer_sem, back_sem, count_sem,
+    load_sem, store_sem, send_sem, far_sem, near_sem, answer_sem, back_sem, count_sem,
 ):
     n = rows * cols
     planes = cols // low
@@ -243,15 +243,23 @@
             pltpu.make_async_copy(ref, ref, sem).wait()
 
     barrier = pltpu.get_barrier_semaphore()
-    for k in range(planes):
-        for j in range(per):
-            if k or j:
-                pl.semaphore_signal(barrier, inc=1, device_id=device(k, j), device_id_type=MESH)
-
-    load_first = pltpu.make_async_copy(first_hbm.at[0], first, weight_sem.at[0])
-    load_second = pltpu.make_async_copy(second_hbm.at[0], second, weight_sem.at[1])
-    load_first.start()
-    load_second.start()
+    near_by = [(0, j) for j in range(1, per)]
+    peers = [(k, 0) for k in far] + near_by
+    for k, j in peers:
+        pl.semaphore_signal(barrier, inc=1, device_id=device(k, j), device_id_type=MESH)
+
+    loads = [
+        pltpu.make_async_copy(source, target, load_sem.at[i])
+        for i, (source, target) in enumerate(
+            (
+                (ids_hbm, ids_row_ref), (tokens_hbm, tokens_ref), (gain_hbm, gain_ref),
+                (gate_hbm, gate_row_ref), (first_hbm.at[0], first), (second_hbm.at[0], second),
+            )
+        )
+    ]
+    for load in loads:
+        load.start()
+    loads[0].wait()
 
     def place_of(ids):
         offset = jnp.bitwise_xor(ids, me)
@@ -275,6 +283,8 @@
     start = jnp.where(plane_t == 0, near_t * cap, ahead.astype(jnp.int32))
     placed_row = plane_t * span + start + within.astype(jnp.int32)
 
+    loads[1].wait()
+    loads[2].wait()
     wide = tokens_ref[...].astype(jnp.float32)
     scale = lax.rsqrt(jnp.mean(wide * wide, axis=1, keepdims=True) + 1e-06)
     normed[...] = (wide * scale * gain_ref[...]).astype(jnp.bfloat16)
@@ -327,7 +337,7 @@
 
     pack(far[0])
     with jax.named_scope("barrier_wait"):
-        pl.semaphore_wait(barrier, n - 1)
+        pl.semaphore_wait(barrier, len(peers))
     for k in far:
         send(counts, counts_far.at[k], send_sem.at[4], count_sem.at[0], device(k, 0))
     send_far(far[0])
@@ -337,22 +347,19 @@
     for k in sent[1:]:
         pack(k)
         send_far(k)
-    for k in range(planes):
-        for j in range(1, per):
-            send(
-                counts, counts_in.at[k * (per - 1) + j - 1], send_sem.at[5], count_sem.at[1],
-                device(k, j),
-            )
-
     def to_column(row, size):
         there = lax.broadcasted_iota(jnp.int32, (size, size), 0)
         here = lax.broadcasted_iota(jnp.int32, (size, size), 1)
         return jnp.sum(jnp.where(there == here, row, 0.0), axis=1, keepdims=True)
 
     placed_col[...] = to_column(placed_row.astype(jnp.float32), tok_rows).astype(jnp.int32)
+    loads[3].wait()
     gate_col[...] = to_column(gate_row_ref[...], tok_rows)
 
     wait(counts_far.at[pl.ds(1, planes - 1)], count_sem.at[0], "wait_counts")
+    sums[...] = counts[...] + jnp.sum(counts_far[pl.ds(1, planes - 1)], axis=0)
+    for k, j in near_by:
+        send(sums, sums_in.at[j], send_sem.at[5], count_sem.at[1], device(k, j))
     expert = lax.broadcasted_iota(jnp.int32, (lanes, span), 0)
     plane_s, near_s = place_of(expert)
     here = (plane_s == 0) & (expert < n)
@@ -370,8 +377,8 @@
         index_col[k] = to_column(index, span).astype(jnp.int32)
 
     with jax.named_scope("wait_weights"):
-        load_first.wait()
-        load_second.wait()
+        loads[4].wait()
+        loads[5].wait()
 
     def relay(k, h):
         wait(packed_in.at[k, h], far_sem.at[k, h], f"wait_far#k={k}#h={h}")
@@ -379,11 +386,12 @@
         table = ones_at(slot == index_col[k])
         fill(k, h, jnp.dot(table, packed_in[k, h], preferred_element_type=jnp.float32))
 
-    def grow(k):
+    def await_slots(k):
         for h in range(parts):
             wait_near(slots_in, near_sem, k, h, "wait_slots")
 
-        @pl.loop(0, first.shape[1] // ff_tile)
+    def grow(k):
+        @pl.loop(0, first.shape[1] // ff_tile, unroll=min(4, first.shape[1] // ff_tile))
         def _(i):
             part = pl.ds(pl.multiple_of(i * ff_tile, ff_tile), ff_tile)
             grown = jnp.dot(slots_in[k, 0], first[columns(0), part], preferred_element_type=jnp.float32)
@@ -394,7 +402,7 @@
             hidden[:, part] = jnp.maximum(grown, 0.0).astype(jnp.bfloat16)
 
     def shrink(k, h):
-        @pl.loop(0, wide_part // out_tile)
+        @pl.loop(0, wide_part // out_tile, unroll=True)
         def _(i):
             at = pl.multiple_of(i * out_tile, out_tile)
             part = pl.ds(pl.multiple_of(h * wide_part + i * out_tile, out_tile), out_tile)
@@ -427,39 +435,40 @@
         return jnp.dot(table, source[k, h], preferred_element_type=jnp.float32)
 
     halves = range(parts)
+    todo = far[:1] + far[:0:-1]
+    await_slots(0)
     grow(0)
     for h in halves:
         shrink(0, h)
-    for h in halves:
-        relay(far[0], h)
-    todo = far[:1] + far[:0:-1]
+    for k in todo[:2]:
+        for h in halves:
+            relay(k, h)
     for i, k in enumerate(todo):
+        await_slots(k)
         grow(k)
-        after = todo[i + 1] if i + 1 < len(todo) else None
-        last = i + 2 == len(todo)
-        if after is not None:
-            relay(after, 0)
-            if last:
-                give_back(todo[i - 1], 0)
-                for h in range(1, parts):
-                    give_back(todo[i - 1], h)
+        behind = todo[i + 1 : i + 2] if i else []
+        for k2 in behind:
+            relay(k2, 0)
+        for h in halves:
+            if i == 1:
+                give_back(todo[0], h)
+        for k2 in behind:
             for h in range(1, parts):
-                relay(after, h)
+                relay(k2, h)
         for h in halves:
-            if after is None and i:
-                give_back(todo[i - 1], h)
             shrink(k, h)
             send_answers(k, h)
+            if i > 1:
+                give_back(todo[i - 1], h)
+    for h in halves:
+        give_back(todo[-1], h)
     for h in halves:
         send_answers(0, h)
-    for h in halves:
-        give_back(todo[-1], h)
-
-    wait(counts_in, count_sem.at[1])
-    sums = jnp.sum(counts_in[...], axis=0) + counts[...]
-    sums += jnp.sum(counts_far[pl.ds(1, planes - 1)], axis=0)
-    routed_ref[0] = jnp.sum(jnp.where(lane == me, sums, 0.0)).astype(jnp.int32)
-    over_ref[0] = jnp.sum(jnp.where(lane == n, sums, 0.0)).astype(jnp.int32)
+
+    wait(sums_in.at[pl.ds(1, per - 1)], count_sem.at[1])
+    whole = sums[...] + jnp.sum(sums_in[pl.ds(1, per - 1)], axis=0)
+    routed_ref[0] = jnp.sum(jnp.where(lane == me, whole, 0.0)).astype(jnp.int32)
+    over_ref[0] = jnp.sum(jnp.where(lane == n, whole, 0.0)).astype(jnp.int32)
 
     for h in range(parts):
         total[h] = picked(0, h)
@@ -470,13 +479,18 @@
         found = total[h] + picked(todo[-1], h)
         kept = tokens_ref[:, columns(h)].astype(jnp.float32)
         mixed_ref[:, columns(h)] = (kept + gate_col[...] * found).astype(jnp.bfloat16)
+        pltpu.make_async_copy(
+            mixed_ref.at[:, columns(h)], mixed_hbm.at[:, columns(h)], store_sem.at[h]
+        ).start()
 
     wait(packed.at[pl.ds(1, planes - 1)], send_sem.at[0])
     wait(slots.at[:, :, pl.ds(cap, span - cap)], send_sem.at[1])
     wait(answers.at[:, :, pl.ds(cap, span - cap)], send_sem.at[2])
     wait(back.at[pl.ds(1, planes - 1)], send_sem.at[3])
     wait(counts_far.at[pl.ds(1, planes - 1)], send_sem.at[4])
-    wait(counts_in, send_sem.at[5])
+    wait(sums_in.at[pl.ds(1, per - 1)], send_sem.at[5])
+    for h in halves:
+        wait(mixed_ref.at[:, columns(h)], store_sem.at[h])
 
 
 def packed_layer(rows, cols, tokens, expert_ids, gate_prob, norm_gain, weight_in, weight_out):
@@ -492,7 +506,6 @@
     parts = 2
     part = width // parts
     lanes = -(-(n + 1) // 128) * 128
-    vmem = pl.BlockSpec(memory_space=pltpu.VMEM)
     smem = pl.BlockSpec(memory_space=pltpu.SMEM)
     hbm = pl.BlockSpec(memory_space=pl.ANY)
     tight = pltpu.VMEM((planes, parts, keep, part), jnp.bfloat16)
@@ -508,9 +521,14 @@
             jax.ShapeDtypeStruct((1,), jnp.int32),
             jax.ShapeDtypeStruct((1,), jnp.int32),
         ),
-        in_specs=[vmem, vmem, vmem, vmem, hbm, hbm],
-        out_specs=(vmem, smem, smem),
+        in_specs=[hbm, hbm, hbm, hbm, hbm, hbm],
+        out_specs=(hbm, smem, smem),
         scratch_shapes=[
+            pltpu.VMEM((tok_rows, width), jnp.bfloat16),
+            pltpu.VMEM((1, tok_rows), jnp.int32),
+            pltpu.VMEM((1, tok_rows), jnp.float32),
+            pltpu.VMEM((1, width), jnp.float32),
+            pltpu.VMEM((tok_rows, width), jnp.bfloat16),
             pltpu.VMEM((width, hidden_width), jnp.bfloat16),
             pltpu.VMEM((hidden_width, width), jnp.bfloat16),
             pltpu.VMEM((tok_rows, width), jnp.bfloat16),
@@ -519,12 +537,14 @@
             pltpu.VMEM((parts, tok_rows, part), jnp.float32),
             pltpu.VMEM((1, lanes), jnp.float32),
             pltpu.VMEM((planes, 1, lanes), jnp.float32),
-            pltpu.VMEM((planes * (per - 1), 1, lanes), jnp.float32),
+            pltpu.VMEM((1, lanes), jnp.float32),
+            pltpu.VMEM((per, 1, lanes), jnp.float32),
             pltpu.VMEM((planes, 1, span), jnp.int32),
             pltpu.VMEM((planes, span, 1), jnp.int32),
             pltpu.VMEM((tok_rows, 1), jnp.int32),
             pltpu.VMEM((tok_rows, 1), jnp.float32),
-            pltpu.SemaphoreType.DMA((2,)),
+            pltpu.SemaphoreType.DMA((6,)),
+            pltpu.SemaphoreType.DMA((parts,)),
             pltpu.SemaphoreType.DMA((6,)),
             each, each, each, each,
             pltpu.SemaphoreType.DMA((2,)),

time: 91.5 us -> 84.2 us (0.920)
  the two profiles are of different devices: /device:TPU:0 before, /device:TPU:9 now
where the time goes in v3:
time: 84.2 us; the launch traced here: 84 us
  Pallas kernels  80 us (95%)
  between operations  3.02 us (4%)
  local copies, waits for them, and re-layouts  0.99 us (1%)
    pallas_call x1, Pallas kernels, packed_layer(): pl.pallas_call(functools.partial(packed_kernel, rows, cols, low, cap, kee...  80 us

profile of v3, /device:TPU:9, one launch (start us, length us, event | category | flops | bytes accessed | tf_op | source)
XLA Modules:
  0.0 84.0 jit_solution(16670827387372508294)
XLA Ops:
  0.6 0.0 copy-start
  0.6 0.0 copy-start.1
  0.6 0.0 copy-start.2
  0.7 0.0 copy-start.3
  0.7 80.0 %shard_map.77 = (bf16[512,1024]{1,0:T(8,128)(2,1)S(1)}, s32[1]{0:T(128)}, s32[1]{0:T(128)}) custom-call(bf16[512,1024]{1,0:T(8,128)(2,1)} %tokens_hbm.1, s32[1,512]{1,0:T(1,128)} %bitcast.9, f32[1,512]{1,0:T(1,128)} %bitcast.8, f32[1,1024]{1,0:T(1,128)} %bitcast.6, bf16[1,1024,4096]{2,1,0:T(8,128)(2,1)} %first_hbm.1, bf16[1,4096,1024]{2,1,0:T(8,128)(2,1)} %second_hbm.1), custom_call_target="tpu_custom_call" | custom-call | tf_op jit(solution)/shard_map/pallas_call | solution.py:514
  81.2 0.0 copy-done
  81.2 0.0 copy-done.1
  81.2 0.0 copy-done.2
  81.2 0.0 copy-done.3
  81.3 1.0 %copy.12 = bf16[512,1024]{1,0:T(8,128)(2,1)} copy(bf16[512,1024]{1,0:T(8,128)(2,1)S(1)} %get-tuple-element.35) | data formatting | bytes 2097152
  (1 shorter events, 0.0 us)
Async XLA Ops:
  0.6 80.6 %copy-start = (bf16[512,1024]{1,0:T(8,128)(2,1)S(1)}, bf16[512,1024]{1,0:T(8,128)(2,1)}, u32[]{:S(2)}) copy-start(bf16[512,1024]{1,0:T(8,128)(2,1)} %tokens_hbm.1) | copy-start | bytes 3145732
  0.6 80.6 %copy-start.1 = (f32[1024]{0:T(1024)S(1)}, f32[1024]{0:T(1024)}, u32[]{:S(2)}) copy-start(f32[1024]{0:T(1024)} %param.11) | copy-start | bytes 12292
  0.6 80.6 %copy-start.2 = (f32[512]{0:T(512)S(1)}, f32[512]{0:T(512)}, u32[]{:S(2)}) copy-start(f32[512]{0:T(512)} %param.10) | copy-start | bytes 6148
  0.7 80.6 %copy-start.3 = (s32[512,1]{0,1:T(1,128)S(1)}, s32[512,1]{0,1:T(1,128)}, u32[]{:S(2)}) copy-start(s32[512,1]{0,1:T(1,128)} %param.9) | copy-start | bytes 6148

commit v4 on v3

--- a/solution.py
+++ b/solution.py
@@ -446,15 +446,12 @@
     for i, k in enumerate(todo):
         await_slots(k)
         grow(k)
-        behind = todo[i + 1 : i + 2] if i else []
-        for k2 in behind:
-            relay(k2, 0)
+        for k2 in todo[i + 1 : i + 2] if i else []:
+            for h in halves:
+                relay(k2, h)
         for h in halves:
             if i == 1:
                 give_back(todo[0], h)
-        for k2 in behind:
-            for h in range(1, parts):
-                relay(k2, h)
         for h in halves:
             shrink(k, h)
             send_answers(k, h)

time: 84.2 us -> 83.4 us (level)
  the two profiles are of different devices: /device:TPU:9 before, /device:TPU:0 now
where the time goes in v4:
time: 83.4 us; the launch traced here: 83.2 us
  Pallas kernels  79.2 us (95%)
  between operations  3.02 us (4%)
  local copies, waits for them, and re-layouts  0.99 us (1%)
    pallas_call x1, Pallas kernels, packed_layer(): pl.pallas_call(functools.partial(packed_kernel, rows, cols, low, cap, kee...  79.2 us

profile of v4, /device:TPU:0, one launch (start us, length us, event | category | flops | bytes accessed | tf_op | source)
XLA Modules:
  0.0 83.2 jit_solution(11913240936201098141)
XLA Ops:
  0.6 0.0 copy-start
  0.6 0.0 copy-start.1
  0.6 0.0 copy-start.2
  0.7 0.0 copy-start.3
  0.7 79.2 %shard_map.77 = (bf16[512,1024]{1,0:T(8,128)(2,1)S(1)}, s32[1]{0:T(128)}, s32[1]{0:T(128)}) custom-call(bf16[512,1024]{1,0:T(8,128)(2,1)} %tokens_hbm.1, s32[1,512]{1,0:T(1,128)} %bitcast.9, f32[1,512]{1,0:T(1,128)} %bitcast.8, f32[1,1024]{1,0:T(1,128)} %bitcast.6, bf16[1,1024,4096]{2,1,0:T(8,128)(2,1)} %first_hbm.1, bf16[1,4096,1024]{2,1,0:T(8,128)(2,1)} %second_hbm.1), custom_call_target="tpu_custom_call" | custom-call | tf_op jit(solution)/shard_map/pallas_call | solution.py:511
  80.5 0.0 copy-done
  80.5 0.0 copy-done.1
  80.5 0.0 copy-done.2
  80.5 0.0 copy-done.3
  80.5 1.0 %copy.12 = bf16[512,1024]{1,0:T(8,128)(2,1)} copy(bf16[512,1024]{1,0:T(8,128)(2,1)S(1)} %get-tuple-element.35) | data formatting | bytes 2097152
  (1 shorter events, 0.0 us)
Async XLA Ops:
  0.6 79.8 %copy-start = (bf16[512,1024]{1,0:T(8,128)(2,1)S(1)}, bf16[512,1024]{1,0:T(8,128)(2,1)}, u32[]{:S(2)}) copy-start(bf16[512,1024]{1,0:T(8,128)(2,1)} %tokens_hbm.1) | copy-start | bytes 3145732
  0.6 79.8 %copy-start.1 = (f32[1024]{0:T(1024)S(1)}, f32[1024]{0:T(1024)}, u32[]{:S(2)}) copy-start(f32[1024]{0:T(1024)} %param.11) | copy-start | bytes 12292
  0.6 79.8 %copy-start.2 = (f32[512]{0:T(512)S(1)}, f32[512]{0:T(512)}, u32[]{:S(2)}) copy-start(f32[512]{0:T(512)} %param.10) | copy-start | bytes 6148
  0.7 79.8 %copy-start.3 = (s32[512,1]{0,1:T(1,128)S(1)}, s32[512,1]{0,1:T(1,128)}, u32[]{:S(2)}) copy-start(s32[512,1]{0,1:T(1,128)} %param.9) | copy-start | bytes 6148

commit v5 on v4

--- a/solution.py
+++ b/solution.py
@@ -203,13 +203,13 @@
 
 
 def packed_kernel(
-    rows, cols, low, cap, keep, parts, ff_tile, out_tile,
+    rows, cols, low, cap, near_keep, main, pool, parts, ff_tile, out_tile,
     tokens_hbm, ids_hbm, gate_hbm, gain_hbm, first_hbm, second_hbm,
     mixed_hbm, routed_ref, over_ref,
     tokens_ref, ids_row_ref, gate_row_ref, gain_ref, mixed_ref, first, second, normed, packed, packed_in, slots, slots_in, answers, answers_in,
-    back, back_in, hidden, total, counts, counts_far, sums, sums_in,
+    back, back_in, pooled, pool_in, pool_out, pool_back, hidden, total, counts, counts_far, sums, sums_in,
     index_row, index_col, placed_col, gate_col,
-    load_sem, store_sem, send_sem, far_sem, near_sem, answer_sem, back_sem, count_sem,
+    load_sem, store_sem, send_sem, far_sem, near_sem, answer_sem, back_sem, pool_sem, merge_sem, count_sem,
 ):
     n = rows * cols
     planes = cols // low
@@ -229,6 +229,14 @@
     if planes % 2:
         sent = far
 
+    pairs = list(range(2, planes, 2))
+
+    def keep_of(k):
+        return near_keep if k == 1 else main
+
+    def pool_row(rank, k):
+        return pool - 1 - (rank - main) if k % 2 else rank - main
+
     def device(k, j):
         return (row_at[j % rows], plane_at[k] + low_at[j // rows])
 
@@ -296,9 +304,13 @@
     lane = lax.broadcasted_iota(jnp.int32, (1, lanes), 1)
     plane_l, _ = place_of(lane)
     over = jnp.zeros((1, 1), jnp.float32)
+    held = [jnp.sum(jnp.where(plane_l == k, tally, 0.0), axis=1, keepdims=True) for k in range(planes)]
     for k in far:
-        held = jnp.sum(jnp.where(plane_l == k, tally, 0.0), axis=1, keepdims=True)
-        over = over + jnp.where(held > keep, 1.0, 0.0)
+        if k == 1:
+            over = over + jnp.where(held[1] > near_keep, 1.0, 0.0)
+        elif k % 2 == 0:
+            extra = jnp.maximum(held[k] - main, 0.0) + jnp.maximum(held[k + 1] - main, 0.0)
+            over = over + jnp.where(extra > pool, 1.0, 0.0)
     counts[...] = tally + jnp.where(lane == n, over, 0.0)
 
     def columns(h):
@@ -308,16 +320,45 @@
         slot = lax.broadcasted_iota(jnp.int32, (size, tok_rows), 0) + k * span
         return ones_at(slot == placed_row)
 
+    def chunk(ref, k, h):
+        return ref.at[k, h, pl.ds(0, keep_of(k))]
+
+    def in_pool(slot, placed, k):
+        first_hit = slot == pool_row(placed - k * span, k)
+        return ones_at(first_hit | (slot == pool_row(placed - (k + 1) * span, k + 1)))
+
     def pack(k):
-        table = gather_from(k, keep)
+        table = gather_from(k, keep_of(k))
         for h in range(parts):
-            packed[k, h] = jnp.dot(
+            packed[k, h, 0 : keep_of(k)] = jnp.dot(
                 table, normed[:, columns(h)], preferred_element_type=jnp.float32
             ).astype(jnp.bfloat16)
 
+    def pack_pool(k):
+        slot = lax.broadcasted_iota(jnp.int32, (pool, tok_rows), 0)
+        table = in_pool(slot, placed_row, k)
+        for h in range(parts):
+            pooled[k // 2, h] = jnp.dot(
+                table, normed[:, columns(h)], preferred_element_type=jnp.float32
+            ).astype(jnp.bfloat16)
+
     def send_far(k):
         for h in range(parts):
-            send(packed.at[k, h], packed_in.at[k, h], send_sem.at[0], far_sem.at[k, h], device(k, 0))
+            send(
+                chunk(packed, k, h), chunk(packed_in, k, h), send_sem.at[0 if k > 1 else 6],
+                far_sem.at[k, h], device(k, 0),
+            )
+            if k > 1 and k % 2:
+                send(
+                    pooled.at[k // 2, h], pool_in.at[k, h], send_sem.at[7], pool_sem.at[k, h],
+                    device(k, 0),
+                )
+
+    def pass_pool(k, h):
+        send(
+            pool_in.at[k, h], pool_in.at[k - 1, h], send_sem.at[8], pool_sem.at[k - 1, h],
+            device(1, 0),
+        )
 
     def send_near(source, target, out_sem, sem, k, h):
         for j in range(1, per):
@@ -335,6 +376,8 @@
         slots[k, h] = made
         send_near(slots, slots_in, send_sem.at[1], near_sem, k, h)
 
+    if pairs:
+        pack_pool(far[0] - 1)
     pack(far[0])
     with jax.named_scope("barrier_wait"):
         pl.semaphore_wait(barrier, len(peers))
@@ -345,6 +388,8 @@
     for h in range(parts):
         fill(0, h, jnp.dot(table, normed[:, columns(h)], preferred_element_type=jnp.float32))
     for k in sent[1:]:
+        if k > 1 and k % 2:
+            pack_pool(k - 1)
         pack(k)
         send_far(k)
     def to_column(row, size):
@@ -381,10 +426,23 @@
         loads[5].wait()
 
     def relay(k, h):
-        wait(packed_in.at[k, h], far_sem.at[k, h], f"wait_far#k={k}#h={h}")
+        wait(chunk(packed_in, k, h), far_sem.at[k, h], f"wait_far#k={k}#h={h}")
+        keep = keep_of(k)
         slot = lax.broadcasted_iota(jnp.int32, (span, keep), 1)
-        table = ones_at(slot == index_col[k])
-        fill(k, h, jnp.dot(table, packed_in[k, h], preferred_element_type=jnp.float32))
+        values = jnp.dot(
+            ones_at(slot == index_col[k]), packed_in[k, h, 0:keep],
+            preferred_element_type=jnp.float32,
+        )
+        if k > 1:
+            wait(pool_in.at[k, h], pool_sem.at[k, h], f"wait_pool#k={k}#h={h}")
+            slot = lax.broadcasted_iota(jnp.int32, (span, pool), 1)
+            values += jnp.dot(
+                ones_at(slot == pool_row(index_col[k], k)), pool_in[k, h],
+                preferred_element_type=jnp.float32,
+            )
+        fill(k, h, values)
+        if k > 1 and k % 2:
+            pass_pool(k, h)
 
     def await_slots(k):
         for h in range(parts):
@@ -401,45 +459,69 @@
                 )
             hidden[:, part] = jnp.maximum(grown, 0.0).astype(jnp.bfloat16)
 
-    def shrink(k, h):
-        @pl.loop(0, wide_part // out_tile, unroll=True)
-        def _(i):
-            at = pl.multiple_of(i * out_tile, out_tile)
-            part = pl.ds(pl.multiple_of(h * wide_part + i * out_tile, out_tile), out_tile)
-            made = jnp.dot(hidden[...], second[:, part], preferred_element_type=jnp.float32)
-            made = made.astype(jnp.bfloat16)
-            answers[k, h, :, pl.ds(at, out_tile)] = made
-            answers_in[k, h, 0:cap, pl.ds(at, out_tile)] = made[0:cap]
+    def shrink(k, group):
+        for h in group:
+            for at in range(0, wide_part, out_tile):
+                part = pl.ds(h * wide_part + at, out_tile)
+                made = jnp.dot(hidden[...], second[:, part], preferred_element_type=jnp.float32)
+                made = made.astype(jnp.bfloat16)
+                answers[k, h, :, at : at + out_tile] = made
+                answers_in[k, h, 0:cap, at : at + out_tile] = made[0:cap]
 
     def send_answers(k, h):
         send_near(answers, answers_in, send_sem.at[2], answer_sem, k, h)
 
     def give_back(k, h):
         wait_near(answers_in, answer_sem, k, h, "wait_answers")
+        keep = keep_of(k)
         slot = lax.broadcasted_iota(jnp.int32, (keep, span), 0)
-        table = ones_at(slot == index_row[k])
-        back[k, h] = jnp.dot(
-            table, answers_in[k, h], preferred_element_type=jnp.float32
+        back[k, h, 0:keep] = jnp.dot(
+            ones_at(slot == index_row[k]), answers_in[k, h], preferred_element_type=jnp.float32
         ).astype(jnp.bfloat16)
-        send(back.at[k, h], back_in.at[k, h], send_sem.at[3], back_sem.at[k, h], device(k, 0))
+        send(
+            chunk(back, k, h), chunk(back_in, k, h), send_sem.at[3 if k > 1 else 9],
+            back_sem.at[k, h], device(k, 0),
+        )
+        if k > 1:
+            slot = lax.broadcasted_iota(jnp.int32, (pool, span), 0)
+            values = jnp.dot(
+                ones_at(slot == pool_row(index_row[k], k)), answers_in[k, h],
+                preferred_element_type=jnp.float32,
+            )
+            if k % 2 == 0:
+                wait(pool_back.at[k + 1, h], merge_sem.at[k + 1, h], f"wait_merge#k={k}#h={h}")
+                values += pool_back[k + 1, h].astype(jnp.float32)
+            pool_out[k, h] = values.astype(jnp.bfloat16)
+            send(
+                pool_out.at[k, h], pool_back.at[k, h], send_sem.at[10], merge_sem.at[k, h],
+                device(1 if k % 2 else k, 0),
+            )
 
     def picked(k, h):
-        size = keep if k else span
         if k:
-            wait(back_in.at[k, h], back_sem.at[k, h], f"wait_back#k={k}#h={h}")
+            wait(chunk(back_in, k, h), back_sem.at[k, h], f"wait_back#k={k}#h={h}")
+            size, source = keep_of(k), back_in
         else:
             wait_near(answers_in, answer_sem, 0, h, "wait_answers")
-        source = back_in if k else answers_in
+            size, source = span, answers_in
         slot = lax.broadcasted_iota(jnp.int32, (tok_rows, size), 1) + k * span
         table = ones_at(slot == placed_col[...])
-        return jnp.dot(table, source[k, h], preferred_element_type=jnp.float32)
+        values = jnp.dot(table, source[k, h, 0:size], preferred_element_type=jnp.float32)
+        if k > 1 and k % 2 == 0:
+            wait(pool_back.at[k, h], merge_sem.at[k, h], f"wait_pool_back#k={k}#h={h}")
+            slot = lax.broadcasted_iota(jnp.int32, (tok_rows, pool), 1)
+            values += jnp.dot(
+                in_pool(slot, placed_col[...], k), pool_back[k, h], preferred_element_type=jnp.float32
+            )
+        return values
 
     halves = range(parts)
     todo = far[:1] + far[:0:-1]
     await_slots(0)
     grow(0)
-    for h in halves:
-        shrink(0, h)
+    groups = [halves[i : i + parts // 2] for i in range(0, parts, parts // 2)]
+    for group in groups:
+        shrink(0, group)
     for k in todo[:2]:
         for h in halves:
             relay(k, h)
@@ -452,11 +534,13 @@
         for h in halves:
             if i == 1:
                 give_back(todo[0], h)
-        for h in halves:
-            shrink(k, h)
-            send_answers(k, h)
-            if i > 1:
-                give_back(todo[i - 1], h)
+        for group in groups:
+            shrink(k, group)
+            for h in group:
+                send_answers(k, h)
+            for h in group:
+                if i > 1:
+                    give_back(todo[i - 1], h)
     for h in halves:
         give_back(todo[-1], h)
     for h in halves:
@@ -480,10 +564,16 @@
             mixed_ref.at[:, columns(h)], mixed_hbm.at[:, columns(h)], store_sem.at[h]
         ).start()
 
-    wait(packed.at[pl.ds(1, planes - 1)], send_sem.at[0])
+    wait(packed.at[1, :, pl.ds(0, near_keep)], send_sem.at[6])
+    wait(back.at[1, :, pl.ds(0, near_keep)], send_sem.at[9])
+    if pairs:
+        wait(packed.at[pl.ds(2, planes - 2), :, pl.ds(0, main)], send_sem.at[0])
+        wait(back.at[pl.ds(2, planes - 2), :, pl.ds(0, main)], send_sem.at[3])
+        wait(pooled.at[pl.ds(1, len(pairs))], send_sem.at[7])
+        wait(pooled.at[pl.ds(1, len(pairs))], send_sem.at[8])
+        wait(pool_out.at[pl.ds(2, planes - 2)], send_sem.at[10])
     wait(slots.at[:, :, pl.ds(cap, span - cap)], send_sem.at[1])
     wait(answers.at[:, :, pl.ds(cap, span - cap)], send_sem.at[2])
-    wait(back.at[pl.ds(1, planes - 1)], send_sem.at[3])
     wait(counts_far.at[pl.ds(1, planes - 1)], send_sem.at[4])
     wait(sums_in.at[pl.ds(1, per - 1)], send_sem.at[5])
     for h in halves:
@@ -499,18 +589,20 @@
     per = n // planes
     cap = 2 * tok_rows // n
     span = per * cap
-    keep = 3 * span // 4
-    parts = 2
+    near_keep, main, pool = (-(-part * span // 256) * 16 for part in (13, 9, 3))
+    parts = 4
     part = width // parts
     lanes = -(-(n + 1) // 128) * 128
     smem = pl.BlockSpec(memory_space=pltpu.SMEM)
     hbm = pl.BlockSpec(memory_space=pl.ANY)
-    tight = pltpu.VMEM((planes, parts, keep, part), jnp.bfloat16)
+    tight = pltpu.VMEM((planes, parts, near_keep, part), jnp.bfloat16)
+    shared = pltpu.VMEM((planes, parts, pool, part), jnp.bfloat16)
+    some = pltpu.VMEM((max(1, planes // 2), parts, pool, part), jnp.bfloat16)
     loose = pltpu.VMEM((planes, parts, span, part), jnp.bfloat16)
     each = pltpu.SemaphoreType.DMA((planes, parts))
     return pl.pallas_call(
         functools.partial(
-            packed_kernel, rows, cols, low, cap, keep, parts,
+            packed_kernel, rows, cols, low, cap, near_keep, main, pool, parts,
             min(512, hidden_width), min(256, part),
         ),
         out_shape=(
@@ -530,6 +622,7 @@
             pltpu.VMEM((hidden_width, width), jnp.bfloat16),
             pltpu.VMEM((tok_rows, width), jnp.bfloat16),
             tight, tight, loose, loose, loose, loose, tight, tight,
+            some, shared, shared, shared,
             pltpu.VMEM((span, hidden_width), jnp.bfloat16),
             pltpu.VMEM((parts, tok_rows, part), jnp.float32),
             pltpu.VMEM((1, lanes), jnp.float32),
@@ -542,8 +635,8 @@
             pltpu.VMEM((tok_rows, 1), jnp.float32),
             pltpu.SemaphoreType.DMA((6,)),
             pltpu.SemaphoreType.DMA((parts,)),
-            pltpu.SemaphoreType.DMA((6,)),
-            each, each, each, each,
+            pltpu.SemaphoreType.DMA((11,)),
+            each, each, each, each, each, each,
             pltpu.SemaphoreType.DMA((2,)),
         ],
         compiler_params=pltpu.CompilerParams(

time: 83.4 us -> 81.6 us (0.978)
  Pallas kernels: 79.2 us -> 77.4 us
    pallas_call x1, Pallas kernels: 79.2 us -> 77.4 us  [packed_layer(): pl.pallas_call(functools.partial(packed_kernel, rows, cols, low, cap, nea...]
where the time goes in v5:
time: 81.6 us; the launch traced here: 81.4 us
  Pallas kernels  77.4 us (95%)
  between operations  3.02 us (4%)
  local copies, waits for them, and re-layouts  0.99 us (1%)
    pallas_call x1, Pallas kernels, packed_layer(): pl.pallas_call(functools.partial(packed_kernel, rows, cols, low, cap, nea...  77.4 us

profile of v5, /device:TPU:0, one launch (start us, length us, event | category | flops | bytes accessed | tf_op | source)
XLA Modules:
  0.0 81.4 jit_solution(13361279456149623551)
XLA Ops:
  0.6 0.0 copy-start
  0.6 0.0 copy-start.1
  0.6 0.0 copy-start.2
  0.7 0.0 copy-start.3
  0.7 77.4 %shard_map.77 = (bf16[512,1024]{1,0:T(8,128)(2,1)S(1)}, s32[1]{0:T(128)}, s32[1]{0:T(128)}) custom-call(bf16[512,1024]{1,0:T(8,128)(2,1)} %tokens_hbm.1, s32[1,512]{1,0:T(1,128)} %bitcast.9, f32[1,512]{1,0:T(1,128)} %bitcast.8, f32[1,1024]{1,0:T(1,128)} %bitcast.6, bf16[1,1024,4096]{2,1,0:T(8,128)(2,1)} %first_hbm.1, bf16[1,4096,1024]{2,1,0:T(8,128)(2,1)} %second_hbm.1), custom_call_target="tpu_custom_call" | custom-call | tf_op jit(solution)/shard_map/pallas_call | solution.py:603
  78.6 0.0 copy-done
  78.6 0.0 copy-done.1
  78.6 0.0 copy-done.2
  78.7 0.0 copy-done.3
  78.7 1.0 %copy.12 = bf16[512,1024]{1,0:T(8,128)(2,1)} copy(bf16[512,1024]{1,0:T(8,128)(2,1)S(1)} %get-tuple-element.35) | data formatting | bytes 2097152
  (1 shorter events, 0.0 us)
Async XLA Ops:
  0.6 78.0 %copy-start = (bf16[512,1024]{1,0:T(8,128)(2,1)S(1)}, bf16[512,1024]{1,0:T(8,128)(2,1)}, u32[]{:S(2)}) copy-start(bf16[512,1024]{1,0:T(8,128)(2,1)} %tokens_hbm.1) | copy-start | bytes 3145732
  0.6 78.0 %copy-start.1 = (f32[1024]{0:T(1024)S(1)}, f32[1024]{0:T(1024)}, u32[]{:S(2)}) copy-start(f32[1024]{0:T(1024)} %param.11) | copy-start | bytes 12292
  0.6 78.0 %copy-start.2 = (f32[512]{0:T(512)S(1)}, f32[512]{0:T(512)}, u32[]{:S(2)}) copy-start(f32[512]{0:T(512)} %param.10) | copy-start | bytes 6148
  0.7 78.0 %copy-start.3 = (s32[512,1]{0,1:T(1,128)S(1)}, s32[512,1]{0,1:T(1,128)}, u32[]{:S(2)}) copy-start(s32[512,1]{0,1:T(1,128)} %param.9) | copy-start | bytes 6148
